TPU v7x, 32 devices: a whole 2x2x4 slice. The times are simulated.
32 devices in a mesh: slab: 8 (over z, core), grp: 4 (over y, x).
Axes of the slice: x: 2, y: 2, z: 4, core: 2. Of those that a mesh axis runs over, the one named last changes fastest.
Arguments:
- comp: float32 [256, 128, 128], P(('slab', 'grp')), may hold values from -1 to 1
- guess: float32 [64, 32, 32], P('slab', 'grp'), may hold values from -3 to 3
Outputs:
- comp_next: float32 [256, 128, 128], P(('slab', 'grp'))
- potential: float32 [64, 32, 32], P('slab', 'grp')
All inputs are finite; a program needn't handle non-finite values.
Results may differ from a plain program's by a relative error of at most 0.00002.
Values sent between devices are 32-bit elements; how exact they have to be, the bound alone decides.
No kernel may reach another device: no remote copies, remote signals or barrier semaphores. Data moves between devices by JAX's collectives and lax.ppermute only.
A program may use at most 64 MiB of HBM per device.

v0:
```python
import jax
import jax.numpy as jnp
from jax import lax
from jax.sharding import PartitionSpec as P

NPRE = 1
NCOARSE = 3
NPOST = 2


gradient_energy = 0.5
screening = 0.5
damping = 0.8
long_range = 4.0
time_step = 0.02


def extended_2(block, sides, width):
    for axis, dim in sides:
        count = lax.axis_size(axis)
        forward = [(i, i + 1) for i in range(count - 1)]
        backward = [(target, source) for source, target in forward]
        low = lax.ppermute(
            lax.slice_in_dim(block, block.shape[dim] - width, None, axis=dim), axis, forward
        )
        high = lax.ppermute(lax.slice_in_dim(block, 0, width, axis=dim), axis, backward)
        block = jnp.concatenate([low, block, high], axis=dim)
    return block


def laplace_padded(padded):
    inner = padded[1:-1, 1:-1, 1:-1]
    beside_all = padded[2:, 1:-1, 1:-1] + padded[:-2, 1:-1, 1:-1]
    beside_all = beside_all + padded[1:-1, 2:, 1:-1] + padded[1:-1, :-2, 1:-1]
    beside_all = beside_all + padded[1:-1, 1:-1, 2:] + padded[1:-1, 1:-1, :-2]
    return beside_all - 6.0 * inner


def pad_across(field):
    return jnp.pad(field, ((0, 0), (1, 1), (1, 1)))


def block_mean(field, factor):
    first, second, third = field.shape
    return field.reshape(
        first // factor, factor, second // factor, factor, third // factor, factor
    ).mean(axis=(1, 3, 5))


def expand(field, factor):
    first, second, third = field.shape
    wide = jnp.broadcast_to(
        field[:, None, :, None, :, None], (first, factor, second, factor, third, factor)
    )
    return wide.reshape(first * factor, second * factor, third * factor)


def keep_inside(field, first_plane, total_planes):
    plane_ids = first_plane + jnp.arange(field.shape[0], dtype=jnp.int32)
    inside = (plane_ids >= 0) & (plane_ids < total_planes)
    return jnp.where(inside[:, None, None], field, jnp.float32(0.0))


def shrink_sweep(potential, source, first_plane, total_planes):
    operated = screening * potential[1:-1] - laplace_padded(pad_across(potential))
    updated = potential[1:-1] + damping * (source[1:-1] - operated) / (screening + 6.0)
    return (keep_inside(updated, first_plane + 1, total_planes), source[1:-1], first_plane + 1)


def deep_cycle(source, guess):
    local_planes = source.shape[0]
    local_rows = guess.shape[1]
    block, start = (
        lax.all_gather(source, "grp", axis=0, tiled=True),
        lax.all_gather(guess, "grp", axis=1, tiled=True),
    )
    group_planes = block.shape[0]
    depth = NPRE + NPOST + 2 * NCOARSE - 1
    total_planes = lax.axis_size("slab") * group_planes
    wide_source, wide_pot = (
        extended_2(block, (("slab", 0),), depth),
        extended_2(start, (("slab", 0),), depth),
    )
    first_plane = lax.axis_index("slab") * group_planes - depth
    wide_pot, wide_source, first_plane = shrink_sweep(
        wide_pot, wide_source, first_plane, total_planes
    )
    operated = screening * wide_pot[1:-1] - laplace_padded(pad_across(wide_pot))
    residual = keep_inside(wide_source[1:-1] - operated, first_plane + 1, total_planes)
    wide_pot = wide_pot[1:-1]
    wide_source = wide_source[1:-1]
    first_plane = first_plane + 1
    coarsest = block_mean(residual, 2)
    coarse_first = first_plane // 2
    coarse_total = total_planes // 2
    correction = damping * coarsest / (screening + 1.5)
    for sweep in range(NCOARSE - 1):
        operated = screening * correction[1:-1] - 0.25 * laplace_padded(pad_across(correction))
        correction = correction[1:-1] + damping * (coarsest[1:-1] - operated) / (screening + 1.5)
        coarse_first = coarse_first + 1
        correction = keep_inside(correction, coarse_first, coarse_total)
        coarsest = coarsest[1:-1]
    cut = 2 * (NCOARSE - 1)
    wide_pot = wide_pot[cut:-cut] + expand(correction, 2)
    wide_source = wide_source[cut:-cut]
    first_plane = first_plane + cut
    for sweep in range(NPOST):
        wide_pot, wide_source, first_plane = shrink_sweep(
            wide_pot, wide_source, first_plane, total_planes
        )
    potential = lax.dynamic_slice_in_dim(
        wide_pot, lax.axis_index("grp") * local_rows, local_rows, 1
    )
    slab_planes = lax.dynamic_slice_in_dim(
        wide_pot, lax.axis_index("grp") * local_planes, local_planes, 0
    )
    return (potential, slab_planes)


def per_device(comp, guess):
    extended = extended_2(comp, ((("slab", "grp"), 0),), 1)
    chem = comp * comp * comp - comp - gradient_energy * laplace_padded(pad_across(extended))
    source = block_mean(comp, 4)
    potential, slab_planes = deep_cycle(source, guess)
    field = chem + long_range * expand(slab_planes, 4)
    extended = extended_2(field, ((("slab", "grp"), 0),), 1)
    comp_next = comp + time_step * laplace_padded(pad_across(extended))
    return (comp_next, potential)


def solution(mesh):
    placed = (P(("slab", "grp"), None, None), P("slab", "grp", None))
    return jax.shard_map(
        per_device,
        mesh=mesh,
        in_specs=placed,
        out_specs=(P(("slab", "grp"), None, None), P("slab", "grp", None)),
        check_vma=False,
    )
```

profile of v0, /device:TPU:8, one launch (start us, length us, event | category | flops | bytes accessed | tf_op | source)
XLA Modules:
  0.0 115.8 jit_solution(10051776300398007658)
XLA Ops:
  0.6 19.5 %reshape.60 = f32[2,4,32,4,32,4]{5,4,3,2,1,0:T(8,128)} reshape(f32[8,128,128]{2,1,0:T(8,128)} %param.2) | data formatting | bytes 1048576 | tf_op jit(solution)/shard_map/reshape | solution.py:45
  20.1 0.0 copy-start.4
  20.1 7.1 %reduce_sum.18 = f32[2,32,32]{2,1,0:T(8,128)S(1)} reduce(f32[2,4,32,4,32,4]{5,4,3,2,1,0:T(8,128)} %reshape.60, f32[]{:T(128)} %constant.36.clone.1), dimensions={1,3,5}, to_apply=%region_0.1 | reduce | flops 129024 | bytes 532484 | tf_op jit(solution)/shard_map/reduce_sum | solution.py:47
  27.2 8.5 %all_gather.7 = f32[8,32,32]{2,1,0:T(8,128)S(1)} all-gather(f32[2,32,32]{2,1,0:T(8,128)S(1)} %broadcast_multiply_fusion.2), channel_id=1, replica_groups=mesh['slab'=8,'grp'=4] {'grp'}, dimensions={0}, use_global_device_ids=true | all-gather | bytes 40960 | tf_op jit(solution)/shard_map/all_gather | solution.py:74
  35.6 0.0 copy-start.2
  35.6 1.9 %collective-permute-start.4 = (f32[8,32,32]{2,1,0:T(8,128)S(1)}, f32[8,32,32]{2,1,0:T(8,128)S(1)}, u32[]{:S(2)}, u32[]{:S(2)}) collective-permute-start(f32[8,32,32]{2,1,0:T(8,128)S(1)} %all_gather.7), channel_id=1, source_target_pairs={{0,4},{4,8},{8,12},{12,16},{16,20},{20,24},{24,28},{1,5},{5,9},{9,... | collective-permute-start | bytes 98312 | tf_op jit(solution)/shard_map/ppermute | solution.py:23
  37.6 3.6 %collective-permute-start.5 = (f32[8,32,32]{2,1,0:T(8,128)S(1)}, f32[8,32,32]{2,1,0:T(8,128)S(1)}, u32[]{:S(2)}, u32[]{:S(2)}) collective-permute-start(f32[8,32,32]{2,1,0:T(8,128)S(1)} %all_gather.7), channel_id=1, source_target_pairs={{4,0},{8,4},{12,8},{16,12},{20,16},{24,20},{28,24},{5,1},{9,5},{13... | collective-permute-start | bytes 98312 | tf_op jit(solution)/shard_map/ppermute | solution.py:26
  41.2 0.0 copy-done.4
  41.2 9.0 %all_gather.6 = f32[8,32,32]{2,1,0:T(8,128)S(1)} all-gather(f32[8,8,32]{2,1,0:T(8,128)S(1)} %copy-done.4), channel_id=1, replica_groups=mesh['slab'=8,'grp'=4] {'grp'}, dimensions={1}, use_global_device_ids=true | all-gather | bytes 40960 | tf_op jit(solution)/shard_map/all_gather | solution.py:75
  50.2 1.9 %collective-permute-start.2 = (f32[8,32,32]{2,1,0:T(8,128)S(1)}, f32[8,32,32]{2,1,0:T(8,128)S(1)}, u32[]{:S(2)}, u32[]{:S(2)}) collective-permute-start(f32[8,32,32]{2,1,0:T(8,128)S(1)} %all_gather.6), channel_id=1, source_target_pairs={{0,4},{4,8},{8,12},{12,16},{16,20},{20,24},{24,28},{1,5},{5,9},{9,... | collective-permute-start | bytes 98312 | tf_op jit(solution)/shard_map/ppermute | solution.py:23
  52.1 3.6 %collective-permute-start.3 = (f32[8,32,32]{2,1,0:T(8,128)S(1)}, f32[8,32,32]{2,1,0:T(8,128)S(1)}, u32[]{:S(2)}, u32[]{:S(2)}) collective-permute-start(f32[8,32,32]{2,1,0:T(8,128)S(1)} %all_gather.6), channel_id=1, source_target_pairs={{4,0},{8,4},{12,8},{16,12},{20,16},{24,20},{28,24},{5,1},{9,5},{13... | collective-permute-start | bytes 98312 | tf_op jit(solution)/shard_map/ppermute | solution.py:26
  55.8 1.5 %fusion.73 = (f32[1,128,128]{2,1,0:T(8,128)}, f32[1,128,128]{2,1,0:T(8,128)}) fusion(f32[8,128,128]{2,1,0:T(8,128)} %param.2), kind=kLoop, calls=%fused_computation.142 | loop fusion | bytes 262144 | tf_op jit(solution)/shard_map/slice | solution.py:24
  57.3 2.8 %collective-permute-start = (f32[1,128,128]{2,1,0:T(8,128)}, f32[1,128,128]{2,1,0:T(8,128)}, u32[]{:S(2)}, u32[]{:S(2)}) collective-permute-start(f32[1,128,128]{2,1,0:T(8,128)} %get-tuple-element.5), channel_id=1, source_target_pairs={{1,0},{2,1},{3,2},{4,3},{5,4},{6,5},{7,6},{8,7},{9,8},{10,9},{11,1... | collective-permute-start | bytes 196616 | tf_op jit(solution)/shard_map/ppermute | solution.py:26
  60.2 0.0 collective-permute-done.4
  60.2 3.0 %collective-permute-start.1 = (f32[1,128,128]{2,1,0:T(8,128)}, f32[1,128,128]{2,1,0:T(8,128)}, u32[]{:S(2)}, u32[]{:S(2)}) collective-permute-start(f32[1,128,128]{2,1,0:T(8,128)} %get-tuple-element.4), channel_id=1, source_target_pairs={{0,1},{1,2},{2,3},{3,4},{4,5},{5,6},{6,7},{7,8},{8,9},{9,10},{10,1... | collective-permute-start | bytes 196616 | tf_op jit(solution)/shard_map/ppermute | solution.py:23
  63.3 0.0 collective-permute-done.2
  63.4 0.0 collective-permute-done.5
  63.4 0.0 copy-start.1
  63.4 0.0 collective-permute-done.3
  63.4 0.0 copy-done.2
  63.4 0.4 fusion.21
  63.8 0.3 copy-done.1
  64.1 0.3 fusion.29
  64.4 4.4 %reshape.61 = f32[10,2,16,2,16,2]{5,4,3,2,1,0:T(8,128)} reshape(f32[20,32,32]{2,1,0:T(8,128)S(1)} %fusion.29) | data formatting | bytes 163840 | tf_op jit(solution)/shard_map/reshape | solution.py:45
  68.8 2.9 %reduce_sum.19 = f32[10,16,16]{2,1,0:T(8,128)S(1)} reduce(f32[10,2,16,2,16,2]{5,4,3,2,1,0:T(8,128)} %reshape.61, f32[]{:T(128)} %constant.36.clone.1), dimensions={1,3,5}, to_apply=%region_1.2 | reduce | flops 17920 | bytes 92164 | tf_op jit(solution)/shard_map/reduce_sum | solution.py:47
  71.8 0.1 fusion.60
  71.9 0.1 fusion.71
  72.0 0.3 broadcast_in_dim.100
  72.3 2.1 %reshape.62 = f32[12,32,32]{2,1,0:T(8,128)} reshape(f32[6,2,16,2,16,2]{5,4,3,2,1,0:T(8,128)S(1)} %broadcast_in_dim.100) | data formatting | bytes 98304 | tf_op jit(solution)/shard_map/reshape | solution.py:55
  74.4 0.0 copy-start.3
  74.4 1.0 slice_add_fusion.10
  75.4 1.1 fusion.39
  76.5 0.0 copy-done.3
  76.5 0.1 fusion.49
  76.7 8.0 %broadcast_in_dim.103 = f32[2,4,32,4,32,4]{5,4,3,2,1,0:T(8,128)} broadcast(f32[2,32,32]{2,1,0:T(8,128)S(1)} %dynamic-slice_multiply_fusion), dimensions={0,2,4} | broadcast | bytes 532480 | tf_op jit(solution)/shard_map/broadcast_in_dim | solution.py:52
  84.6 0.0 copy-start
  84.6 14.8 %mul.176 = f32[8,128,128]{2,1,0:T(8,128)S(1)} reshape(f32[2,4,32,4,32,4]{5,4,3,2,1,0:T(8,128)} %broadcast_in_dim.103) | data formatting | bytes 1048576 | tf_op jit(solution)/shard_map/mul | solution.py:125
  99.5 0.0 collective-permute-done
  99.5 0.0 collective-permute-done.1
  99.5 0.0 copy-done
  99.5 1.3 %select_maximum_fusion.2 = f32[10,130,130]{2,1,0:T(8,128)S(1)} fusion(f32[1,128,128]{2,1,0:T(8,128)} %collective-permute-done, f32[8,128,128]{2,1,0:T(8,128)S(1)} %copy-done, f32[1,128,128]{2,1,0:T(8,128)} %collective-permute-done.1), kind=kLoop, calls=%fused_computation.6 | loop fusion | flops 2535000 | bytes 1331360 | tf_op jit(solution)/shard_map/concatenate | solution.py:27
  100.8 1.5 %fusion.4 = f32[8,128,128]{2,1,0:T(8,128)S(1)} fusion(f32[8,128,128]{2,1,0:T(8,128)S(1)} %mul.176, f32[8,128,128]{2,1,0:T(8,128)S(1)} %copy-done, f32[10,130,130]{2,1,0:T(8,128)S(1)} %select_maximum_fusion.2, f32[1,128,128]{2,1,0:T(8,128)} %collective-permute-done.1, f32[1,128,128]{2,1,0:T(8,128)} %collective-permute-done), kind=kLoop, calls=%fused_computation.17 | loop fusion | flops 1966080 | bytes 3801088 | tf_op jit(solution)/shard_map/add | solution.py:125
  102.3 4.3 %collective-permute-start.6 = (f32[1,128,128]{2,1,0:T(8,128)S(1)}, f32[1,128,128]{2,1,0:T(8,128)S(1)}, u32[]{:S(2)}, u32[]{:S(2)}) collective-permute-start(f32[1,128,128]{2,1,0:T(8,128)S(1)} %get-tuple-element.3), channel_id=1, source_target_pairs={{1,0},{2,1},{3,2},{4,3},{5,4},{6,5},{7,6},{8,7},{9,8},{10,9},{11,1... | collective-permute-start | bytes 196616 | tf_op jit(solution)/shard_map/ppermute | solution.py:26
  106.7 1.9 %collective-permute-start.7 = (f32[1,128,128]{2,1,0:T(8,128)S(1)}, f32[1,128,128]{2,1,0:T(8,128)S(1)}, u32[]{:S(2)}, u32[]{:S(2)}) collective-permute-start(f32[1,128,128]{2,1,0:T(8,128)S(1)} %get-tuple-element.2), channel_id=1, source_target_pairs={{0,1},{1,2},{2,3},{3,4},{4,5},{5,6},{6,7},{7,8},{8,9},{9,10},{10,1... | collective-permute-start | bytes 196616 | tf_op jit(solution)/shard_map/ppermute | solution.py:23
  108.6 0.6 constant_dynamic-slice_fusion
  109.2 0.0 collective-permute-done.6
  109.2 4.8 %collective-permute-done.7 = f32[1,128,128]{2,1,0:T(8,128)S(1)} collective-permute-done((f32[1,128,128]{2,1,0:T(8,128)S(1)}, f32[1,128,128]{2,1,0:T(8,128)S(1)}, u32[]{:S(2)}, u32[]{:S(2)}) %collective-permute-start.7) | collective-permute-done | bytes 65568 | tf_op jit(solution)/shard_map/ppermute | solution.py:23
  114.1 0.4 select_maximum_fusion
  114.5 1.3 %fusion.7 = f32[8,128,128]{2,1,0:T(8,128)} fusion(f32[8,128,128]{2,1,0:T(8,128)S(1)} %copy-done, f32[10,130,130]{2,1,0:T(8,128)S(1)} %select_maximum_fusion, f32[8,128,128]{2,1,0:T(8,128)S(1)} %fusion.4, f32[1,128,128]{2,1,0:T(8,128)S(1)} %collective-permute-done.7, f32[1,128,128]{2,1,0:T(8,128)S(1)} %collective-permute-done.6), kind=kLoop, calls=%fused_computation.21 | loop fusion | flops 1441792 | bytes 3801088 | tf_op jit(solution)/shard_map/add | solution.py:127
  (16 shorter events, 0.2 us)
Async XLA Ops:
  20.1 21.1 %copy-start.4 = (f32[8,8,32]{2,1,0:T(8,128)S(1)}, f32[8,8,32]{2,1,0:T(8,128)}, u32[]{:S(2)}) copy-start(f32[8,8,32]{2,1,0:T(8,128)} %param.3) | copy-start | bytes 24580
  35.6 27.8 %copy-start.2 = (f32[8,32,32]{2,1,0:T(8,128)}, f32[8,32,32]{2,1,0:T(8,128)S(1)}, u32[]{:S(2)}) copy-start(f32[8,32,32]{2,1,0:T(8,128)S(1)} %all_gather.7) | copy-start | bytes 98308
  35.6 24.6 %collective-permute-start.4 = (f32[8,32,32]{2,1,0:T(8,128)S(1)}, f32[8,32,32]{2,1,0:T(8,128)S(1)}, u32[]{:S(2)}, u32[]{:S(2)}) collective-permute-start(f32[8,32,32]{2,1,0:T(8,128)S(1)} %all_gather.7), channel_id=1, source_target_pairs={{0,4},{4,8},{8,12},{12,16},{16,20},{20,24},{24,28},{1,5},{5,9},{9,... | collective-permute-start | bytes 98312 | tf_op jit(solution)/shard_map/ppermute | solution.py:23
  37.6 25.8 %collective-permute-start.5 = (f32[8,32,32]{2,1,0:T(8,128)S(1)}, f32[8,32,32]{2,1,0:T(8,128)S(1)}, u32[]{:S(2)}, u32[]{:S(2)}) collective-permute-start(f32[8,32,32]{2,1,0:T(8,128)S(1)} %all_gather.7), channel_id=1, source_target_pairs={{4,0},{8,4},{12,8},{16,12},{20,16},{24,20},{28,24},{5,1},{9,5},{13... | collective-permute-start | bytes 98312 | tf_op jit(solution)/shard_map/ppermute | solution.py:26
  50.2 13.1 %collective-permute-start.2 = (f32[8,32,32]{2,1,0:T(8,128)S(1)}, f32[8,32,32]{2,1,0:T(8,128)S(1)}, u32[]{:S(2)}, u32[]{:S(2)}) collective-permute-start(f32[8,32,32]{2,1,0:T(8,128)S(1)} %all_gather.6), channel_id=1, source_target_pairs={{0,4},{4,8},{8,12},{12,16},{16,20},{20,24},{24,28},{1,5},{5,9},{9,... | collective-permute-start | bytes 98312 | tf_op jit(solution)/shard_map/ppermute | solution.py:23
  52.1 11.3 %collective-permute-start.3 = (f32[8,32,32]{2,1,0:T(8,128)S(1)}, f32[8,32,32]{2,1,0:T(8,128)S(1)}, u32[]{:S(2)}, u32[]{:S(2)}) collective-permute-start(f32[8,32,32]{2,1,0:T(8,128)S(1)} %all_gather.6), channel_id=1, source_target_pairs={{4,0},{8,4},{12,8},{16,12},{20,16},{24,20},{28,24},{5,1},{9,5},{13... | collective-permute-start | bytes 98312 | tf_op jit(solution)/shard_map/ppermute | solution.py:26
  57.3 42.2 %collective-permute-start = (f32[1,128,128]{2,1,0:T(8,128)}, f32[1,128,128]{2,1,0:T(8,128)}, u32[]{:S(2)}, u32[]{:S(2)}) collective-permute-start(f32[1,128,128]{2,1,0:T(8,128)} %get-tuple-element.5), channel_id=1, source_target_pairs={{1,0},{2,1},{3,2},{4,3},{5,4},{6,5},{7,6},{8,7},{9,8},{10,9},{11,1... | collective-permute-start | bytes 196616 | tf_op jit(solution)/shard_map/ppermute | solution.py:26
  60.2 39.2 %collective-permute-start.1 = (f32[1,128,128]{2,1,0:T(8,128)}, f32[1,128,128]{2,1,0:T(8,128)}, u32[]{:S(2)}, u32[]{:S(2)}) collective-permute-start(f32[1,128,128]{2,1,0:T(8,128)} %get-tuple-element.4), channel_id=1, source_target_pairs={{0,1},{1,2},{2,3},{3,4},{4,5},{5,6},{6,7},{7,8},{8,9},{9,10},{10,1... | collective-permute-start | bytes 196616 | tf_op jit(solution)/shard_map/ppermute | solution.py:23
  63.4 0.7 copy-start.1
  74.4 2.1 %copy-start.3 = (f32[8,32,32]{2,1,0:T(8,128)S(1)}, f32[8,32,32]{2,1,0:T(8,128)}, u32[]{:S(2)}) copy-start(f32[8,32,32]{2,1,0:T(8,128)} %copy-done.2) | copy-start | bytes 98308
  84.6 14.9 %copy-start = (f32[8,128,128]{2,1,0:T(8,128)S(1)}, f32[8,128,128]{2,1,0:T(8,128)}, u32[]{:S(2)}) copy-start(f32[8,128,128]{2,1,0:T(8,128)} %param.2) | copy-start | bytes 1572868
  102.3 6.9 %collective-permute-start.6 = (f32[1,128,128]{2,1,0:T(8,128)S(1)}, f32[1,128,128]{2,1,0:T(8,128)S(1)}, u32[]{:S(2)}, u32[]{:S(2)}) collective-permute-start(f32[1,128,128]{2,1,0:T(8,128)S(1)} %get-tuple-element.3), channel_id=1, source_target_pairs={{1,0},{2,1},{3,2},{4,3},{5,4},{6,5},{7,6},{8,7},{9,8},{10,9},{11,1... | collective-permute-start | bytes 196616 | tf_op jit(solution)/shard_map/ppermute | solution.py:26
  106.7 7.4 %collective-permute-start.7 = (f32[1,128,128]{2,1,0:T(8,128)S(1)}, f32[1,128,128]{2,1,0:T(8,128)S(1)}, u32[]{:S(2)}, u32[]{:S(2)}) collective-permute-start(f32[1,128,128]{2,1,0:T(8,128)S(1)} %get-tuple-element.2), channel_id=1, source_target_pairs={{0,1},{1,2},{2,3},{3,4},{4,5},{5,6},{6,7},{7,8},{8,9},{9,10},{10,1... | collective-permute-start | bytes 196616 | tf_op jit(solution)/shard_map/ppermute | solution.py:23
where the time goes:
time: 116 us
  local copies, waits for them, and re-layouts  51.6 us (44%)
  starting transfers between devices  23.2 us (20%)
  other arithmetic  17.7 us (15%)
  blocking collectives  17.4 us (15%)
  waiting for transfers between devices  4.84 us (4%)
    reshape x2, local copies, waits for them, and re-layouts, block_mean(): field.reshape(first // factor, factor, second // factor, factor, third //...  23.8 us
    mul x1, local copies, waits for them, and re-layouts, per_device(): field = chem + long_range * expand(slab_planes, 4)  14.8 us
    ppermute x4, starting transfers between devices, extended_2(): lax.ppermute(lax.slice_in_dim(block, 0, width, axis=dim), axis, backward)  14.4 us
    reduce_sum x2, other arithmetic, block_mean(): return field.reshape(first // factor, factor, second // factor, factor, t...  10 us
    all_gather x1, blocking collectives, deep_cycle(): lax.all_gather(guess, 'grp', axis=1, tiled=True)  8.96 us
    ppermute x4, starting transfers between devices, extended_2(): lax.ppermute(lax.slice_in_dim(block, block.shape[dim] - width, None, axis...  8.77 us
    all_gather x1, blocking collectives, deep_cycle(): lax.all_gather(source, 'grp', axis=0, tiled=True)  8.46 us
    broadcast_in_dim x2, local copies, waits for them, and re-layouts, expand(): jnp.broadcast_to(field[:, None, :, None, :, None], (first, factor, second...  8.23 us
  transfers between devices with their start and end apart: 8, of which 1 were waited for; matrix products, arithmetic and copies ran while one was open for 33% of the time, Pallas kernels for 0%

commit v1 on v0

v1 whole, which is shorter than its diff:
```python
import functools

import jax
import jax.numpy as jnp
from jax import lax
from jax.experimental import pallas as pl
from jax.experimental.pallas import tpu as pltpu
from jax.sharding import PartitionSpec as P

NPRE = 1
NCOARSE = 3
NPOST = 2

gradient_energy = 0.5
screening = 0.5
damping = 0.8
long_range = 4.0
time_step = 0.02

LANES = 128
QUAD = 4
HALO = 3

VMEM = pl.BlockSpec(memory_space=pltpu.VMEM)


def lanes_of(shape):
    return lax.broadcasted_iota(jnp.int32, shape, len(shape) - 1)


def rows_of(shape):
    return lax.broadcasted_iota(jnp.int32, shape, len(shape) - 2)


def exact_dot(a, b):
    return jnp.dot(a, b, preferred_element_type=jnp.float32, precision=lax.Precision.HIGHEST)


def pack_kernel(comp_ref, guess_ref, message_ref, first_ref, second_ref):
    columns = guess_ref.shape[2]
    rows = comp_ref.shape[1] // 4
    half = rows // 2
    pooled = []
    for plane in range(comp_ref.shape[0] // 4):
        total = None
        for i in range(4):
            for j in range(4):
                part = comp_ref[4 * plane + i, pl.ds(j, rows, stride=4), :]
                total = part if total is None else total + part
        pooled.append(total)
    stacked = jnp.concatenate(
        [pooled[0][:half], pooled[1][:half], pooled[0][half:], pooled[1][half:]], axis=0
    )
    square = (comp_ref.shape[2], LANES)
    pool = jnp.where(rows_of(square) // 4 == lanes_of(square) % columns, 1.0 / 64.0, 0.0)
    spread = exact_dot(stacked, pool.astype(jnp.float32))
    where = lanes_of((half, LANES)) // columns
    packed = spread[:half]
    for block in range(1, QUAD):
        packed = jnp.where(where == block, spread[block * half : (block + 1) * half], packed)
    message_ref[0:half, :] = packed
    planes, block_rows = guess_ref.shape[0], guess_ref.shape[1]
    for quad in range(planes // QUAD):
        at = half + quad * block_rows
        for i in range(QUAD):
            message_ref[at : at + block_rows, i * columns : (i + 1) * columns] = guess_ref[
                QUAD * quad + i
            ]
    odd = lax.rem(lax.axis_index("grp"), 2)
    top = comp_ref.shape[0] - 2
    first_ref[...] = comp_ref[pl.ds(top * (1 - odd), 2)]
    second_ref[...] = comp_ref[pl.ds(top * odd, 2)]


def pack(comp, guess):
    outer = jax.ShapeDtypeStruct((2,) + comp.shape[1:], jnp.float32)
    message = jax.ShapeDtypeStruct((32, LANES), jnp.float32)
    return pl.pallas_call(
        pack_kernel,
        out_shape=(message, outer, outer),
        in_specs=[VMEM] * 2,
        out_specs=(VMEM,) * 3,
        cost_estimate=pl.CostEstimate(flops=2_000_000, bytes_accessed=800_000, transcendentals=0),
        name="pack",
    )(comp, guess)


def beside_in_plane(v):
    rows, lanes = rows_of(v.shape), lanes_of(v.shape)
    last_row, last_lane = v.shape[0] - 1, v.shape[1] - 1
    total = jnp.where(rows == 0, 0.0, pltpu.roll(v, 1, 0))
    total = total + jnp.where(rows == last_row, 0.0, pltpu.roll(v, last_row, 0))
    total = total + jnp.where(lanes == 0, 0.0, pltpu.roll(v, 1, 1))
    return total + jnp.where(lanes == last_lane, 0.0, pltpu.roll(v, last_lane, 1))


def base_kernel(comp_ref, first_ref, second_ref, base_ref, chem_ref):
    planes = comp_ref.shape[0]
    group, groups = lax.axis_index("grp"), lax.axis_size("grp")
    index = lax.axis_index("slab") * groups + group
    devices = lax.axis_size("slab") * groups
    odd = lax.rem(group, 2) == 1

    def plane(f):
        if f < 0:
            return jnp.where(odd, first_ref[f + 2], second_ref[f + 2])
        if f >= planes:
            return jnp.where(odd, second_ref[f - planes], first_ref[f - planes])
        return comp_ref[f]

    for f in range(-1, planes + 1):
        c = plane(f)
        beside = beside_in_plane(c) + plane(f - 1) + plane(f + 1)
        chem = c * c * c - c - gradient_energy * (beside - 6.0 * c)
        if f < 0:
            chem = jnp.where(index > 0, chem, 0.0)
        if f >= planes:
            chem = jnp.where(index < devices - 1, chem, 0.0)
        chem_ref[f + 1] = chem
    for f in range(planes):
        v = chem_ref[f + 1]
        beside = beside_in_plane(v) + chem_ref[f] + chem_ref[f + 2]
        base_ref[f] = comp_ref[f] + time_step * (beside - 6.0 * v)


def base_of(comp, first, second):
    return pl.pallas_call(
        base_kernel,
        out_shape=jax.ShapeDtypeStruct(comp.shape, jnp.float32),
        in_specs=[VMEM] * 3,
        out_specs=VMEM,
        scratch_shapes=[pltpu.VMEM((comp.shape[0] + 2,) + comp.shape[1:], jnp.float32)],
        cost_estimate=pl.CostEstimate(flops=6_000_000, bytes_accessed=1_500_000, transcendentals=0),
        name="base",
    )(comp, first, second)


def along(v, quad, step):
    shift = (-32 * step) % LANES
    here = pltpu.roll(v[quad], shift, 1)
    other = quad + (1 if step > 0 else -1)
    lanes = lanes_of(here.shape)
    own = lanes < LANES - 32 * step if step > 0 else lanes >= -32 * step
    if 0 <= other < len(v):
        return jnp.where(own, here, pltpu.roll(v[other], shift, 1))
    return jnp.where(own, here, 0.0)


def beside(v, quad, step):
    here = v[quad]
    rows, columns = rows_of(here.shape), lanes_of(here.shape) % 32
    total = along(v, quad, step) + along(v, quad, -step)
    total = total + jnp.where(rows < step, 0.0, pltpu.roll(here, step, 0))
    total = total + jnp.where(rows >= 32 - step, 0.0, pltpu.roll(here, 32 - step, 0))
    total = total + jnp.where(columns < step, 0.0, pltpu.roll(here, step, 1))
    return total + jnp.where(columns >= 32 - step, 0.0, pltpu.roll(here, LANES - step, 1))


def operated(v, quad):
    return screening * v[quad] - (beside(v, quad, 1) - 6.0 * v[quad])


def cell_mean(v):
    rows, lanes = rows_of(v.shape), lanes_of(v.shape)
    v = v + jnp.where(lanes % 2 == 0, pltpu.roll(v, LANES - 1, 1), pltpu.roll(v, 1, 1))
    v = v + jnp.where(
        (lanes // 32) % 2 == 0, pltpu.roll(v, LANES - 32, 1), pltpu.roll(v, 32, 1)
    )
    v = v + jnp.where(rows % 2 == 0, pltpu.roll(v, 31, 0), pltpu.roll(v, 1, 0))
    return v * 0.125


def cycle_kernel(edged, *refs):
    base_ref, own_ref, core_ref, chip_ref = refs[:4]
    refs = refs[4:]
    if edged:
        edge_ref, refs = refs[0], refs[1:]
    next_ref, potential_ref, guess_s, window_s = refs
    groups = lax.axis_size("grp")
    slab, slabs, group = lax.axis_index("slab"), lax.axis_size("slab"), lax.axis_index("grp")
    quads = groups // 2
    block = 32 // groups
    low_half = lanes_of((16, LANES)) < 64
    odd = lax.rem(slab, 2) == 1

    def low(*at):
        return jnp.where(odd, core_ref[at], chip_ref[at])

    def high(*at):
        return jnp.where(odd, chip_ref[at], core_ref[at])

    def own(*at):
        return own_ref[at]

    def source_of(even, uneven):
        top = jnp.where(low_half, even, pltpu.roll(uneven, 64, 1))
        bottom = jnp.where(low_half, pltpu.roll(even, 64, 1), uneven)
        return jnp.concatenate([top, bottom], axis=0)

    source, count = [], 0

    def take(read, quad):
        nonlocal count
        source.append(source_of(read(2 * quad, pl.ds(0, 16)), read(2 * quad + 1, pl.ds(0, 16))))
        for g in range(groups):
            guess_s[count, g * block : (g + 1) * block] = read(
                g, pl.ds(16 + quad * block, block)
            )
        count += 1

    def take_edge():
        nonlocal count
        source.append(source_of(edge_ref[0:16], edge_ref[16:32]))
        guess_s[count] = edge_ref[32:64]
        count += 1

    near = HALO - 1 if edged else HALO
    if edged:
        take_edge()
    for quad in range(quads - near, quads):
        take(low, quad)
    for quad in range(quads):
        take(own, quad)
    for quad in range(near):
        take(high, quad)
    if edged:
        take_edge()
    total = quads + 2 * HALO

    inside = []
    for quad in range(total):
        away = quad - HALO
        if away < 0:
            reach = -(away // quads)
            inside.append(jnp.where(slab >= reach, 1.0, 0.0))
        elif away >= quads:
            inside.append(jnp.where(slab + away // quads < slabs, 1.0, 0.0))
        else:
            inside.append(None)

    def kept(v, quad):
        return v if inside[quad] is None else v * inside[quad]

    guess = [guess_s[quad] for quad in range(total)]
    scale = damping / (screening + 6.0)
    pre = [
        kept(guess[quad] + scale * (source[quad] - operated(guess, quad)), quad)
        for quad in range(total)
    ]
    coarsest = [
        kept(cell_mean(source[quad] - operated(pre, quad)), quad) for quad in range(1, total - 1)
    ]
    scale_b = damping / (screening + 1.5)
    correction = [scale_b * v for v in coarsest]
    for sweep in range(NCOARSE - 1):
        last = sweep == NCOARSE - 2
        updated = []
        for quad in range(len(correction)):
            if last and quad in (0, len(correction) - 1):
                updated.append(None)
                continue
            c = correction[quad]
            applied = screening * c - 0.25 * (beside(correction, quad, 2) - 6.0 * c)
            updated.append(kept(c + scale_b * (coarsest[quad] - applied), quad + 1))
        correction = updated
    found = [pre[quad] + correction[quad - 1] for quad in range(2, total - 2)]
    for sweep in range(NPOST):
        found = [
            kept(v + scale * (source[quad + 2] - operated(found, quad)), quad + 2)
            for quad, v in enumerate(found)
        ]

    for quad in range(len(found)):
        window_s[quad] = found[quad]
    for quad in range(quads):
        rows = window_s[quad + 1, pl.ds(pl.multiple_of(group * block, block), block), :]
        for i in range(QUAD):
            potential_ref[QUAD * quad + i] = rows[:, 32 * i : 32 * (i + 1)]

    picked = []
    for i in range(4):
        at = 2 * group + 3 + i
        picked.append(
            pltpu.roll(window_s[at // QUAD], lax.rem(LANES - 32 * lax.rem(at, QUAD), LANES), 1)
        )
    square = (LANES, LANES)
    widen = jnp.where(rows_of(square) == lanes_of(square) // 4, 1.0, 0.0).astype(jnp.float32)
    wide = exact_dot(jnp.concatenate(picked, axis=0), widen)
    wide = [wide[32 * i : 32 * (i + 1)] for i in range(4)]
    factor = time_step * long_range
    rows, lanes = rows_of((32, LANES)), lanes_of((32, LANES))
    for coarse in range(2):
        here = wide[coarse + 1]
        across = jnp.where(lanes == 0, 0.0, pltpu.roll(here, 1, 1))
        across = across + jnp.where(lanes == LANES - 1, 0.0, pltpu.roll(here, LANES - 1, 1))
        middle = factor * (across - 2.0 * here)
        before = middle + factor * (jnp.where(rows == 0, 0.0, pltpu.roll(here, 1, 0)) - here)
        after = middle + factor * (jnp.where(rows == 31, 0.0, pltpu.roll(here, 31, 0)) - here)
        down = factor * (wide[coarse] - here)
        up = factor * (wide[coarse + 2] - here)
        for f in range(4):
            for j in range(4):
                term = (before, middle, middle, after)[j]
                if f == 0:
                    term = term + down
                if f == 3:
                    term = term + up
                at = (4 * coarse + f, pl.ds(j, 32, stride=4), slice(None))
                next_ref[at] = base_ref[at] + term


def cycle(base, own, core, chip, edge, guess):
    groups = own.shape[0]
    total = groups // 2 + 2 * HALO
    operands = [base, own, core, chip] + ([] if edge is None else [edge])
    return pl.pallas_call(
        functools.partial(cycle_kernel, edge is not None),
        out_shape=(
            jax.ShapeDtypeStruct(base.shape, jnp.float32),
            jax.ShapeDtypeStruct(guess.shape, jnp.float32),
        ),
        in_specs=[VMEM] * len(operands),
        out_specs=(VMEM, VMEM),
        scratch_shapes=[
            pltpu.VMEM((total, 32, LANES), jnp.float32),
            pltpu.VMEM((total - 4, 32, LANES), jnp.float32),
        ],
        cost_estimate=pl.CostEstimate(flops=6_000_000, bytes_accessed=1_500_000, transcendentals=0),
        name="cycle",
    )(*operands)


def per_device(comp, guess):
    slabs, groups = lax.axis_size("slab"), lax.axis_size("grp")
    group = lax.axis_index("grp")
    both = ("slab", "grp")
    devices = slabs * groups
    quads = groups // 2

    message, first, second = pack(comp, guess)

    bundle = jnp.zeros((groups,) + message.shape, jnp.float32)
    bundle = lax.dynamic_update_slice(bundle, message[None], (group, 0, 0))
    received = [
        lax.ppermute(message, "grp", [(i, i ^ k) for i in range(groups)]) for k in range(1, groups)
    ]
    for k, block in enumerate(received, 1):
        bundle = lax.dynamic_update_slice(bundle, block[None], (group ^ k, 0, 0))

    first = lax.ppermute(first, both, [(d, d ^ 1) for d in range(devices)])
    second = lax.ppermute(
        second, both, [p for d in range(1, devices - 1, 2) for p in ((d, d + 1), (d + 1, d))]
    )

    core = lax.ppermute(bundle, "slab", [(i, i ^ 1) for i in range(slabs)])
    chip = lax.ppermute(
        bundle, "slab", [p for i in range(1, slabs - 1, 2) for p in ((i, i + 1), (i + 1, i))]
    )
    edge = None
    if quads < HALO:
        block = 32 // groups
        is_first = group == 0
        edge = jnp.concatenate(
            [
                jnp.where(is_first, bundle[groups - 2 :, :16], bundle[:2, :16]).reshape(32, LANES),
                jnp.where(
                    is_first,
                    bundle[:, 16 + (quads - 1) * block : 16 + quads * block],
                    bundle[:, 16 : 16 + block],
                ).reshape(32, LANES),
            ],
            axis=0,
        )
        pairs = []
        for i in range(slabs - 2):
            pairs.append((i * groups, (i + 2) * groups))
            pairs.append(((i + 2) * groups + groups - 1, i * groups + groups - 1))
        edge = lax.ppermute(edge, both, pairs)

    base = base_of(comp, first, second)
    return cycle(base, bundle, core, chip, edge, guess)


def solution(mesh):
    placed = (P(("slab", "grp"), None, None), P("slab", "grp", None))
    return jax.shard_map(
        per_device,
        mesh=mesh,
        in_specs=placed,
        out_specs=placed,
        check_vma=False,
    )
```

time: 116 us -> 27.7 us (0.24)
  the two profiles are of different devices: /device:TPU:8 before, /device:TPU:0 now
where the time goes in v1:
time: 27.7 us; the launch traced here: 27.5 us
  starting transfers between devices  15 us (54%)
  Pallas kernels  7.91 us (29%)
  local copies, waits for them, and re-layouts  3.24 us (12%)
  between operations  0.77 us (3%)
  waiting for transfers between devices  0.55 us (2%)
    ppermute x3, starting transfers between devices, per_device(): lax.ppermute(message, 'grp', [(i, i ^ k) for i in range(groups)])  4.49 us
    ppermute x1, starting transfers between devices, per_device(): core = lax.ppermute(bundle, 'slab', [(i, i ^ 1) for i in range(slabs)])  3.74 us
    ppermute x1, starting transfers between devices, per_device(): edge = lax.ppermute(edge, both, pairs)  3.47 us
    pallas_call x1, Pallas kernels, cycle(): pl.pallas_call(functools.partial(cycle_kernel, edge is not None), out_sha...  3.41 us
    unnamed x14, local copies, waits for them, and re-layouts  3.22 us
    pallas_call x1, Pallas kernels, base_of(): pl.pallas_call(base_kernel, out_shape=jax.ShapeDtypeStruct(comp.shape, jn...  2.66 us
    ppermute x1, starting transfers between devices, per_device(): first = lax.ppermute(first, both, [(d, d ^ 1) for d in range(devices)])  1.97 us
    pallas_call x1, Pallas kernels, pack(): pl.pallas_call(pack_kernel, out_shape=(message, outer, outer), in_specs=[...  1.84 us
  transfers between devices with their start and end apart: 8, of which 1 were waited for; matrix products, arithmetic and copies ran while one was open for 0% of the time, Pallas kernels for 10%

profile of v1, /device:TPU:0, one launch (start us, length us, event | category | flops | bytes accessed | tf_op | source)
XLA Modules:
  0.0 27.5 jit_solution(17454524652290853245)
XLA Ops:
  0.6 1.8 %pack.1 = (f32[32,128]{1,0:T(8,128)}, f32[2,128,128]{2,1,0:T(8,128)}, f32[2,128,128]{2,1,0:T(8,128)}) custom-call(f32[8,128,128]{2,1,0:T(8,128)} %comp_ref.3, f32[8,8,32]{2,1,0:T(8,128)} %guess_ref.1), custom_call_target="tpu_custom_call" | custom-call | flops 2000000 | bytes 800000 | tf_op jit(solution)/shard_map/pack/pallas_call | solution.py:78
  2.5 3.9 %collective-permute-start.4 = (f32[32,128]{1,0:T(8,128)}, f32[32,128]{1,0:T(8,128)S(1)}, u32[]{:S(2)}, u32[]{:S(2)}) collective-permute-start(f32[32,128]{1,0:T(8,128)} %get-tuple-element.7), channel_id=1, source_target_pairs={{0,3},{1,2},{2,1},{3,0},{4,7},{5,6},{6,5},{7,4},{8,11},{9,10},{10,... | collective-permute-start | bytes 49160 | tf_op jit(solution)/shard_map/ppermute | solution.py:345
  6.4 0.5 %collective-permute-start.3 = (f32[32,128]{1,0:T(8,128)}, f32[32,128]{1,0:T(8,128)S(1)}, u32[]{:S(2)}, u32[]{:S(2)}) collective-permute-start(f32[32,128]{1,0:T(8,128)} %get-tuple-element.7), channel_id=1, source_target_pairs={{0,2},{1,3},{2,0},{3,1},{4,6},{5,7},{6,4},{7,5},{8,10},{9,11},{10,... | collective-permute-start | bytes 49160 | tf_op jit(solution)/shard_map/ppermute | solution.py:345
  6.9 0.1 collective-permute-start.2
  7.0 2.0 %collective-permute-start = (f32[2,128,128]{2,1,0:T(8,128)}, f32[2,128,128]{2,1,0:T(8,128)S(1)}, u32[]{:S(2)}, u32[]{:S(2)}) collective-permute-start(f32[2,128,128]{2,1,0:T(8,128)} %get-tuple-element.5), channel_id=1, source_target_pairs={{0,1},{1,0},{2,3},{3,2},{4,5},{5,4},{6,7},{7,6},{8,9},{9,8},{10,11... | collective-permute-start | bytes 393224 | tf_op jit(solution)/shard_map/ppermute | solution.py:350
  8.9 0.7 %collective-permute-start.1 = (f32[2,128,128]{2,1,0:T(8,128)}, f32[2,128,128]{2,1,0:T(8,128)S(1)}, u32[]{:S(2)}, u32[]{:S(2)}) collective-permute-start(f32[2,128,128]{2,1,0:T(8,128)} %get-tuple-element.6), channel_id=1, source_target_pairs={{1,2},{2,1},{3,4},{4,3},{5,6},{6,5},{7,8},{8,7},{9,10},{10,9},{11,... | collective-permute-start | bytes 393224 | tf_op jit(solution)/shard_map/ppermute | solution.py:351
  9.6 0.0 copy-start.6
  9.6 0.7 %copy-done.6 = f32[32,128]{1,0:T(8,128)S(1)} copy-done((f32[32,128]{1,0:T(8,128)S(1)}, f32[32,128]{1,0:T(8,128)}, u32[]{:S(2)}) %copy-start.6) | copy-done | bytes 16408
  10.3 0.5 %collective-permute-done.2 = f32[32,128]{1,0:T(8,128)S(1)} collective-permute-done((f32[32,128]{1,0:T(8,128)}, f32[32,128]{1,0:T(8,128)S(1)}, u32[]{:S(2)}, u32[]{:S(2)}) %collective-permute-start.2) | collective-permute-done | bytes 16416 | tf_op jit(solution)/shard_map/ppermute | solution.py:345
  10.9 0.0 collective-permute-done.3
  10.9 0.0 collective-permute-done.4
  10.9 0.0 copy-start
  10.9 0.7 %collective-permute-start.6 = (f32[4,32,128]{2,1,0:T(8,128)S(1)}, f32[4,32,128]{2,1,0:T(8,128)S(1)}, u32[]{:S(2)}, u32[]{:S(2)}) collective-permute-start(f32[4,32,128]{2,1,0:T(8,128)S(1)} %bitcast_dynamic-update-slice_fusion.refs_1_), channel_id=1, source_target_pairs={{4,8},{8,4},{12,16},{16,12},{20,24},{24,20},{5,9},{9,5},{13,17},{1... | collective-permute-start | bytes 196616 | tf_op jit(solution)/shard_map/ppermute | solution.py:356
  11.6 3.7 %collective-permute-start.5 = (f32[4,32,128]{2,1,0:T(8,128)S(1)}, f32[4,32,128]{2,1,0:T(8,128)S(1)}, u32[]{:S(2)}, u32[]{:S(2)}) collective-permute-start(f32[4,32,128]{2,1,0:T(8,128)S(1)} %bitcast_dynamic-update-slice_fusion.refs_1_), channel_id=1, source_target_pairs={{0,4},{4,0},{8,12},{12,8},{16,20},{20,16},{24,28},{28,24},{1,5},{5... | collective-permute-start | bytes 196616 | tf_op jit(solution)/shard_map/ppermute | solution.py:355
  15.4 0.0 copy-done
  15.4 3.5 %collective-permute-start.7 = (f32[64,128]{1,0:T(8,128)S(1)}, f32[64,128]{1,0:T(8,128)S(1)}, u32[]{:S(2)}, u32[]{:S(2)}) collective-permute-start(f32[64,128]{1,0:T(8,128)S(1)} %pad_maximum_fusion), channel_id=1, source_target_pairs={{0,8},{11,3},{4,12},{15,7},{8,16},{19,11},{12,20},{23,15},{16,24},... | collective-permute-start | bytes 98312 | tf_op jit(solution)/shard_map/ppermute | solution.py:378
  18.8 0.0 collective-permute-done.first_ref
  18.8 0.0 copy-start.1
  18.9 0.0 collective-permute-done.1.second_ref
  18.9 0.6 %copy-done.1 = f32[2,128,128]{2,1,0:T(8,128)} copy-done((f32[2,128,128]{2,1,0:T(8,128)}, f32[2,128,128]{2,1,0:T(8,128)S(1)}, u32[]{:S(2)}) %copy-start.1) | copy-done | bytes 131096
  19.5 0.0 copy-start.2
  19.5 0.6 %copy-done.2 = f32[2,128,128]{2,1,0:T(8,128)} copy-done((f32[2,128,128]{2,1,0:T(8,128)}, f32[2,128,128]{2,1,0:T(8,128)S(1)}, u32[]{:S(2)}) %copy-start.2) | copy-done | bytes 131096
  20.2 2.7 %base.1.refs_0_ = f32[8,128,128]{2,1,0:T(8,128)} custom-call(f32[8,128,128]{2,1,0:T(8,128)} %comp_ref.3, f32[2,128,128]{2,1,0:T(8,128)} %copy-done.1, f32[2,128,128]{2,1,0:T(8,128)} %copy-done.2), custom_call_target="tpu_custom_call" | custom-call | flops 6000000 | bytes 1500000 | tf_op jit(solution)/shard_map/base/pallas_call | solution.py:127
  22.8 0.0 collective-permute-done.7.refs_4_
  22.8 0.0 copy-start.5
  22.8 0.0 collective-permute-done.6.refs_3_
  22.8 0.0 copy-start.3
  22.8 0.0 collective-permute-done.5.refs_2_
  22.8 0.6 %copy-done.5 = f32[64,128]{1,0:T(8,128)} copy-done((f32[64,128]{1,0:T(8,128)}, f32[64,128]{1,0:T(8,128)S(1)}, u32[]{:S(2)}) %copy-start.5) | copy-done | bytes 32792
  23.4 0.0 copy-done.3
  23.4 0.0 copy-start.4
  23.5 0.6 %copy-done.4 = f32[4,32,128]{2,1,0:T(8,128)} copy-done((f32[4,32,128]{2,1,0:T(8,128)}, f32[4,32,128]{2,1,0:T(8,128)S(1)}, u32[]{:S(2)}) %copy-start.4) | copy-done | bytes 65560
  24.1 3.4 %cycle.1 = (f32[8,128,128]{2,1,0:T(8,128)}, f32[8,8,32]{2,1,0:T(8,128)}) custom-call(f32[8,128,128]{2,1,0:T(8,128)} %base.1.refs_0_, f32[4,32,128]{2,1,0:T(8,128)} %copy-done, f32[4,32,128]{2,1,0:T(8,128)} %copy-done.4, f32[4,32,128]{2,1,0:T(8,128)} %copy-done.3, f32[64,128]{1,0:T(8,128)} %copy-done.5), custom_call_target="tpu_custom_call" | custom-call | flops 6000000 | bytes 1500000 | tf_op jit(solution)/shard_map/cycle/pallas_call | solution.py:316
  (8 shorter events, 0.0 us)
Async XLA Ops:
  2.5 8.4 %collective-permute-start.4 = (f32[32,128]{1,0:T(8,128)}, f32[32,128]{1,0:T(8,128)S(1)}, u32[]{:S(2)}, u32[]{:S(2)}) collective-permute-start(f32[32,128]{1,0:T(8,128)} %get-tuple-element.7), channel_id=1, source_target_pairs={{0,3},{1,2},{2,1},{3,0},{4,7},{5,6},{6,5},{7,4},{8,11},{9,10},{10,... | collective-permute-start | bytes 49160 | tf_op jit(solution)/shard_map/ppermute | solution.py:345
  6.4 4.5 %collective-permute-start.3 = (f32[32,128]{1,0:T(8,128)}, f32[32,128]{1,0:T(8,128)S(1)}, u32[]{:S(2)}, u32[]{:S(2)}) collective-permute-start(f32[32,128]{1,0:T(8,128)} %get-tuple-element.7), channel_id=1, source_target_pairs={{0,2},{1,3},{2,0},{3,1},{4,6},{5,7},{6,4},{7,5},{8,10},{9,11},{10,... | collective-permute-start | bytes 49160 | tf_op jit(solution)/shard_map/ppermute | solution.py:345
  6.9 3.9 %collective-permute-start.2 = (f32[32,128]{1,0:T(8,128)}, f32[32,128]{1,0:T(8,128)S(1)}, u32[]{:S(2)}, u32[]{:S(2)}) collective-permute-start(f32[32,128]{1,0:T(8,128)} %get-tuple-element.7), channel_id=1, source_target_pairs={{0,1},{1,0},{2,3},{3,2},{4,5},{5,4},{6,7},{7,6},{8,9},{9,8},{10,11... | collective-permute-start | bytes 49160 | tf_op jit(solution)/shard_map/ppermute | solution.py:345
  7.0 11.9 %collective-permute-start = (f32[2,128,128]{2,1,0:T(8,128)}, f32[2,128,128]{2,1,0:T(8,128)S(1)}, u32[]{:S(2)}, u32[]{:S(2)}) collective-permute-start(f32[2,128,128]{2,1,0:T(8,128)} %get-tuple-element.5), channel_id=1, source_target_pairs={{0,1},{1,0},{2,3},{3,2},{4,5},{5,4},{6,7},{7,6},{8,9},{9,8},{10,11... | collective-permute-start | bytes 393224 | tf_op jit(solution)/shard_map/ppermute | solution.py:350
  8.9 9.9 %collective-permute-start.1 = (f32[2,128,128]{2,1,0:T(8,128)}, f32[2,128,128]{2,1,0:T(8,128)S(1)}, u32[]{:S(2)}, u32[]{:S(2)}) collective-permute-start(f32[2,128,128]{2,1,0:T(8,128)} %get-tuple-element.6), channel_id=1, source_target_pairs={{1,2},{2,1},{3,4},{4,3},{5,6},{6,5},{7,8},{8,7},{9,10},{10,9},{11,... | collective-permute-start | bytes 393224 | tf_op jit(solution)/shard_map/ppermute | solution.py:351
  9.6 0.7 %copy-start.6 = (f32[32,128]{1,0:T(8,128)S(1)}, f32[32,128]{1,0:T(8,128)}, u32[]{:S(2)}) copy-start(f32[32,128]{1,0:T(8,128)} %get-tuple-element.7) | copy-start | bytes 49156
  10.9 4.5 %copy-start = (f32[4,32,128]{2,1,0:T(8,128)}, f32[4,32,128]{2,1,0:T(8,128)S(1)}, u32[]{:S(2)}) copy-start(f32[4,32,128]{2,1,0:T(8,128)S(1)} %bitcast_dynamic-update-slice_fusion.refs_1_) | copy-start | bytes 196612
  10.9 11.9 %collective-permute-start.6 = (f32[4,32,128]{2,1,0:T(8,128)S(1)}, f32[4,32,128]{2,1,0:T(8,128)S(1)}, u32[]{:S(2)}, u32[]{:S(2)}) collective-permute-start(f32[4,32,128]{2,1,0:T(8,128)S(1)} %bitcast_dynamic-update-slice_fusion.refs_1_), channel_id=1, source_target_pairs={{4,8},{8,4},{12,16},{16,12},{20,24},{24,20},{5,9},{9,5},{13,17},{1... | collective-permute-start | bytes 196616 | tf_op jit(solution)/shard_map/ppermute | solution.py:356
  11.6 11.2 %collective-permute-start.5 = (f32[4,32,128]{2,1,0:T(8,128)S(1)}, f32[4,32,128]{2,1,0:T(8,128)S(1)}, u32[]{:S(2)}, u32[]{:S(2)}) collective-permute-start(f32[4,32,128]{2,1,0:T(8,128)S(1)} %bitcast_dynamic-update-slice_fusion.refs_1_), channel_id=1, source_target_pairs={{0,4},{4,0},{8,12},{12,8},{16,20},{20,16},{24,28},{28,24},{1,5},{5... | collective-permute-start | bytes 196616 | tf_op jit(solution)/shard_map/ppermute | solution.py:355
  15.4 7.5 %collective-permute-start.7 = (f32[64,128]{1,0:T(8,128)S(1)}, f32[64,128]{1,0:T(8,128)S(1)}, u32[]{:S(2)}, u32[]{:S(2)}) collective-permute-start(f32[64,128]{1,0:T(8,128)S(1)} %pad_maximum_fusion), channel_id=1, source_target_pairs={{0,8},{11,3},{4,12},{15,7},{8,16},{19,11},{12,20},{23,15},{16,24},... | collective-permute-start | bytes 98312 | tf_op jit(solution)/shard_map/ppermute | solution.py:378
  18.8 0.7 %copy-start.1 = (f32[2,128,128]{2,1,0:T(8,128)}, f32[2,128,128]{2,1,0:T(8,128)S(1)}, u32[]{:S(2)}) copy-start(f32[2,128,128]{2,1,0:T(8,128)S(1)} %collective-permute-done.first_ref) | copy-start | bytes 393220
  19.5 0.6 %copy-start.2 = (f32[2,128,128]{2,1,0:T(8,128)}, f32[2,128,128]{2,1,0:T(8,128)S(1)}, u32[]{:S(2)}) copy-start(f32[2,128,128]{2,1,0:T(8,128)S(1)} %collective-permute-done.1.second_ref) | copy-start | bytes 393220
  22.8 0.6 %copy-start.5 = (f32[64,128]{1,0:T(8,128)}, f32[64,128]{1,0:T(8,128)S(1)}, u32[]{:S(2)}) copy-start(f32[64,128]{1,0:T(8,128)S(1)} %collective-permute-done.7.refs_4_) | copy-start | bytes 98308
  22.8 0.6 %copy-start.3 = (f32[4,32,128]{2,1,0:T(8,128)}, f32[4,32,128]{2,1,0:T(8,128)S(1)}, u32[]{:S(2)}) copy-start(f32[4,32,128]{2,1,0:T(8,128)S(1)} %collective-permute-done.6.refs_3_) | copy-start | bytes 196612
  23.4 0.6 %copy-start.4 = (f32[4,32,128]{2,1,0:T(8,128)}, f32[4,32,128]{2,1,0:T(8,128)S(1)}, u32[]{:S(2)}) copy-start(f32[4,32,128]{2,1,0:T(8,128)S(1)} %collective-permute-done.5.refs_2_) | copy-start | bytes 196612

commit v2 on v1

v2 whole, which is shorter than its diff:
```python
import functools

import jax
import jax.numpy as jnp
from jax import lax
from jax.experimental import pallas as pl
from jax.experimental.pallas import tpu as pltpu
from jax.sharding import PartitionSpec as P

NCOARSE = 3
NPOST = 2

gradient_energy = 0.5
screening = 0.5
damping = 0.8
long_range = 4.0
time_step = 0.02

LANES = 128
QUAD = 4
HALO = 3

VMEM = pl.BlockSpec(memory_space=pltpu.VMEM)
PARAMS = pltpu.CompilerParams(vmem_limit_bytes=8 * 2**20)


def lanes_of(shape):
    return lax.broadcasted_iota(jnp.int32, shape, len(shape) - 1)


def rows_of(shape):
    return lax.broadcasted_iota(jnp.int32, shape, len(shape) - 2)


def exact_dot(a, b):
    return jnp.dot(a, b, preferred_element_type=jnp.float32, precision=lax.Precision.HIGHEST)


def pack_guess_kernel(guess_ref, packed_ref):
    planes, rows, columns = guess_ref.shape
    for quad in range(planes // QUAD):
        at = quad * rows
        for i in range(QUAD):
            packed_ref[at : at + rows, i * columns : (i + 1) * columns] = guess_ref[QUAD * quad + i]


def pack_guess(guess):
    return pl.pallas_call(
        pack_guess_kernel,
        out_shape=jax.ShapeDtypeStruct((16, LANES), jnp.float32),
        in_specs=[VMEM],
        out_specs=VMEM,
        cost_estimate=pl.CostEstimate(flops=10_000, bytes_accessed=40_000, transcendentals=0),
        compiler_params=PARAMS,
        name="pack_guess",
    )(guess)


def pack_kernel(comp_ref, guess_ref, message_ref, first_ref, second_ref):
    columns = 32
    rows = comp_ref.shape[1] // 4
    half = rows // 2
    message_ref[half:, :] = guess_ref[...]
    pooled = []
    for plane in range(comp_ref.shape[0] // 4):
        total = None
        for i in range(4):
            for j in range(4):
                part = comp_ref[4 * plane + i, pl.ds(j, rows, stride=4), :]
                total = part if total is None else total + part
        pooled.append(total)
    stacked = jnp.concatenate(
        [pooled[0][:half], pooled[1][:half], pooled[0][half:], pooled[1][half:]], axis=0
    )
    square = (comp_ref.shape[2], LANES)
    pool = jnp.where(rows_of(square) // 4 == lanes_of(square) % columns, 1.0 / 64.0, 0.0)
    spread = exact_dot(stacked, pool.astype(jnp.float32))
    where = lanes_of((half, LANES)) // columns
    packed = spread[:half]
    for block in range(1, QUAD):
        packed = jnp.where(where == block, spread[block * half : (block + 1) * half], packed)
    message_ref[0:half, :] = packed
    odd = lax.rem(lax.axis_index("grp"), 2)
    top = comp_ref.shape[0] - 2
    first_ref[...] = comp_ref[pl.ds(top * (1 - odd), 2)]
    second_ref[...] = comp_ref[pl.ds(top * odd, 2)]


def pack(comp, guess):
    outer = jax.ShapeDtypeStruct((2,) + comp.shape[1:], jnp.float32)
    message = jax.ShapeDtypeStruct((32, LANES), jnp.float32)
    return pl.pallas_call(
        pack_kernel,
        out_shape=(message, outer, outer),
        in_specs=[VMEM] * 2,
        out_specs=(VMEM,) * 3,
        cost_estimate=pl.CostEstimate(flops=2_000_000, bytes_accessed=800_000, transcendentals=0),
        compiler_params=PARAMS,
        name="pack",
    )(comp, pack_guess(guess))


def beside_in_plane(v):
    rows, lanes = rows_of(v.shape), lanes_of(v.shape)
    last_row, last_lane = v.shape[0] - 1, v.shape[1] - 1
    total = jnp.where(rows == 0, 0.0, pltpu.roll(v, 1, 0))
    total = total + jnp.where(rows == last_row, 0.0, pltpu.roll(v, last_row, 0))
    total = total + jnp.where(lanes == 0, 0.0, pltpu.roll(v, 1, 1))
    return total + jnp.where(lanes == last_lane, 0.0, pltpu.roll(v, last_lane, 1))


def base_kernel(comp_ref, first_ref, second_ref, base_ref, chem_ref):
    planes = comp_ref.shape[0]
    group, groups = lax.axis_index("grp"), lax.axis_size("grp")
    index = lax.axis_index("slab") * groups + group
    devices = lax.axis_size("slab") * groups
    odd = lax.rem(group, 2) == 1

    def plane(f):
        if f < 0:
            return jnp.where(odd, first_ref[f + 2], second_ref[f + 2])
        if f >= planes:
            return jnp.where(odd, second_ref[f - planes], first_ref[f - planes])
        return comp_ref[f]

    for f in range(-1, planes + 1):
        c = plane(f)
        beside = beside_in_plane(c) + plane(f - 1) + plane(f + 1)
        chem = c * c * c - c - gradient_energy * (beside - 6.0 * c)
        if f < 0:
            chem = jnp.where(index > 0, chem, 0.0)
        if f >= planes:
            chem = jnp.where(index < devices - 1, chem, 0.0)
        chem_ref[f + 1] = chem
    for f in range(planes):
        v = chem_ref[f + 1]
        beside = beside_in_plane(v) + chem_ref[f] + chem_ref[f + 2]
        base_ref[f] = comp_ref[f] + time_step * (beside - 6.0 * v)


def base_of(comp, first, second):
    return pl.pallas_call(
        base_kernel,
        out_shape=jax.ShapeDtypeStruct(comp.shape, jnp.float32),
        in_specs=[VMEM] * 3,
        out_specs=VMEM,
        scratch_shapes=[pltpu.VMEM((comp.shape[0] + 2,) + comp.shape[1:], jnp.float32)],
        cost_estimate=pl.CostEstimate(flops=6_000_000, bytes_accessed=1_500_000, transcendentals=0),
        compiler_params=PARAMS,
        name="base",
    )(comp, first, second)


def along(v, quad, step):
    shift = (-32 * step) % LANES
    here = pltpu.roll(v[quad], shift, 1)
    other = quad + (1 if step > 0 else -1)
    lanes = lanes_of(here.shape)
    own = lanes < LANES - 32 * step if step > 0 else lanes >= -32 * step
    if 0 <= other < len(v):
        return jnp.where(own, here, pltpu.roll(v[other], shift, 1))
    return jnp.where(own, here, 0.0)


def beside(v, quad, step):
    here = v[quad]
    rows, columns = rows_of(here.shape), lanes_of(here.shape) % 32
    total = along(v, quad, step) + along(v, quad, -step)
    total = total + jnp.where(rows < step, 0.0, pltpu.roll(here, step, 0))
    total = total + jnp.where(rows >= 32 - step, 0.0, pltpu.roll(here, 32 - step, 0))
    total = total + jnp.where(columns < step, 0.0, pltpu.roll(here, step, 1))
    return total + jnp.where(columns >= 32 - step, 0.0, pltpu.roll(here, LANES - step, 1))


def operated(v, quad):
    return screening * v[quad] - (beside(v, quad, 1) - 6.0 * v[quad])


def pair_sum(v, step, axis):
    index = (rows_of(v.shape), lanes_of(v.shape))[axis] // step
    other = v.shape[axis] - step
    return v + jnp.where(index % 2 == 0, pltpu.roll(v, other, axis), pltpu.roll(v, step, axis))


def square_sum(v):
    return pair_sum(pair_sum(v, 1, 1), 1, 0)


def cell_mean(v):
    return square_sum(pair_sum(v, 32, 1)) * 0.125


def in_plane(v):
    rows, columns = rows_of(v.shape), lanes_of(v.shape) % 32
    total = jnp.where(rows == 0, 0.0, pltpu.roll(v, 1, 0))
    total = total + jnp.where(rows == 31, 0.0, pltpu.roll(v, 31, 0))
    total = total + jnp.where(columns == 0, 0.0, pltpu.roll(v, 1, 1))
    return total + jnp.where(columns == 31, 0.0, pltpu.roll(v, LANES - 1, 1))


def source_of(even, uneven):
    low_half = lanes_of((16, LANES)) < 64
    top = jnp.where(low_half, even, pltpu.roll(uneven, 64, 1))
    bottom = jnp.where(low_half, pltpu.roll(even, 64, 1), uneven)
    return jnp.concatenate([top, bottom], axis=0)


def widen():
    square = (LANES, LANES)
    return jnp.where(rows_of(square) == lanes_of(square) // 4, 1.0, 0.0).astype(jnp.float32)


scale = damping / (screening + 6.0)
scale_b = damping / (screening + 1.5)
factor = time_step * long_range
edge_share = 0.125 * scale_b * (0.25 * scale_b) ** 2 * scale**2 * factor


def edge_kernel(own_ref, edge_ref, guess_s):
    groups, group = lax.axis_size("grp"), lax.axis_index("grp")
    quads, block = groups // 2, 32 // groups
    up = group == 0
    at = 16 + jnp.where(up, (quads - 1) * block, 0)
    for g in range(groups):
        guess_s[g * block : (g + 1) * block] = own_ref[g, pl.ds(pl.multiple_of(at, block), block)]
    guess = guess_s[...]
    source = jnp.where(
        up,
        source_of(own_ref[groups - 2, 0:16], own_ref[groups - 1, 0:16]),
        source_of(own_ref[0, 0:16], own_ref[1, 0:16]),
    )
    inner = jnp.where(up, pltpu.roll(guess, 32, 1), pltpu.roll(guess, LANES - 32, 1))
    flat = in_plane(guess)
    pre = guess + scale * (source - (screening * guess - (flat + inner - 6.0 * guess)))
    value = square_sum(pre + scale * (flat - (screening + 5.0) * guess))
    value = jnp.where(up, pltpu.roll(value, 32, 1), value)
    edge_ref[...] = edge_share * exact_dot(value, widen())


def edge_of(own):
    return pl.pallas_call(
        edge_kernel,
        out_shape=jax.ShapeDtypeStruct((32, LANES), jnp.float32),
        in_specs=[VMEM],
        out_specs=VMEM,
        scratch_shapes=[pltpu.VMEM((32, LANES), jnp.float32)],
        cost_estimate=pl.CostEstimate(flops=500_000, bytes_accessed=80_000, transcendentals=0),
        compiler_params=PARAMS,
        name="edge",
    )(own)


def solve_kernel(edged, own_ref, core_ref, chip_ref, wide_ref, rows_ref, guess_s, window_s):
    groups = lax.axis_size("grp")
    slab, slabs, group = lax.axis_index("slab"), lax.axis_size("slab"), lax.axis_index("grp")
    quads = groups // 2
    block = 32 // groups
    odd = lax.rem(slab, 2) == 1

    def low(*at):
        return jnp.where(odd, core_ref[at], chip_ref[at])

    def high(*at):
        return jnp.where(odd, chip_ref[at], core_ref[at])

    def own(*at):
        return own_ref[at]

    source = []

    def take(read, quad):
        at = len(source)
        source.append(source_of(read(2 * quad, pl.ds(0, 16)), read(2 * quad + 1, pl.ds(0, 16))))
        for g in range(groups):
            guess_s[at, g * block : (g + 1) * block] = read(g, pl.ds(16 + quad * block, block))

    near, trim = (quads, 0) if edged else (HALO, 1)
    for quad in range(quads - near, quads):
        take(low, quad)
    for quad in range(quads):
        take(own, quad)
    for quad in range(near):
        take(high, quad)
    total = quads + 2 * near
    has_low = jnp.where(slab > 0, 1.0, 0.0)
    has_high = jnp.where(slab < slabs - 1, 1.0, 0.0)

    def kept(v, quad):
        if quad < near:
            return v * has_low
        return v if quad < near + quads else v * has_high

    guess = [guess_s[quad] for quad in range(total)]
    pre = [
        kept(guess[quad] + scale * (source[quad] - operated(guess, quad)), quad)
        for quad in range(total)
    ]
    coarsest = [
        kept(cell_mean(source[quad] - operated(pre, quad)), quad)
        for quad in range(trim, total - trim)
    ]
    correction = [scale_b * v for v in coarsest]
    for sweep in range(NCOARSE - 1):
        last = sweep == NCOARSE - 2
        updated = []
        for quad in range(len(correction)):
            if last and quad in (0, len(correction) - 1):
                updated.append(None)
                continue
            c = correction[quad]
            applied = screening * c - 0.25 * (beside(correction, quad, 2) - 6.0 * c)
            updated.append(kept(c + scale_b * (coarsest[quad] - applied), quad + trim))
        correction = updated
    start = near - 1
    found = [pre[quad] + correction[quad - trim] for quad in range(start, total - start)]
    for _ in range(NPOST):
        found = [
            kept(v + scale * (source[quad + start] - operated(found, quad)), quad + start)
            for quad, v in enumerate(found)
        ]

    for quad in range(len(found)):
        window_s[quad] = found[quad]
    for quad in range(quads):
        rows_ref[quad] = window_s[quad + 1, pl.ds(pl.multiple_of(group * block, block), block), :]

    picked = []
    for i in range(4):
        at = 2 * group + 3 + i
        picked.append(
            pltpu.roll(window_s[at // QUAD], lax.rem(LANES - 32 * lax.rem(at, QUAD), LANES), 1)
        )
    if edged:
        lowest = group == 0
        facing = jnp.where(lowest, guess[0], pltpu.roll(guess[total - 1], 32, 1))
        reach = jnp.where(lowest, slab, slabs - 1 - slab) >= 2
        picked.append(jnp.where(reach, edge_share * scale / factor, 0.0) * square_sum(facing))
    wide = factor * exact_dot(jnp.concatenate(picked, axis=0), widen())
    wide = [wide[32 * i : 32 * (i + 1)] for i in range(len(picked))]
    if edged:
        wide[0] = wide[0] + jnp.where(group == 0, 1.0, 0.0) * wide[4]
        wide[3] = wide[3] + jnp.where(group == groups - 1, 1.0, 0.0) * wide[4]
    for i in range(4):
        wide_ref[i] = wide[i]


def solve(own, core, chip, guess, edged):
    groups = own.shape[0]
    quads = groups // 2
    total = 3 * quads if edged else quads + 2 * HALO
    return pl.pallas_call(
        functools.partial(solve_kernel, edged),
        out_shape=(
            jax.ShapeDtypeStruct((4, 32, LANES), jnp.float32),
            jax.ShapeDtypeStruct((quads, guess.shape[1], LANES), jnp.float32),
        ),
        in_specs=[VMEM] * 3,
        out_specs=(VMEM, VMEM),
        scratch_shapes=[
            pltpu.VMEM((total, 32, LANES), jnp.float32),
            pltpu.VMEM((quads + 2, 32, LANES), jnp.float32),
        ],
        cost_estimate=pl.CostEstimate(flops=6_000_000, bytes_accessed=500_000, transcendentals=0),
        compiler_params=PARAMS,
        name="solve",
    )(own, core, chip)


def finish_kernel(base_ref, wide_ref, rows_ref, *refs):
    edge_ref = refs[0] if len(refs) == 3 else None
    next_ref, potential_ref = refs[-2:]
    group, groups = lax.axis_index("grp"), lax.axis_size("grp")
    for quad in range(rows_ref.shape[0]):
        for i in range(QUAD):
            potential_ref[QUAD * quad + i] = rows_ref[quad, :, 32 * i : 32 * (i + 1)]
    wide = [wide_ref[i] for i in range(4)]
    if edge_ref is not None:
        wide[0] = wide[0] + jnp.where(group == 0, 1.0, 0.0) * edge_ref[...]
        wide[3] = wide[3] + jnp.where(group == groups - 1, 1.0, 0.0) * edge_ref[...]
    rows, lanes = rows_of((32, LANES)), lanes_of((32, LANES))
    for coarse in range(2):
        here = wide[coarse + 1]
        across = jnp.where(lanes == 0, 0.0, pltpu.roll(here, 1, 1))
        across = across + jnp.where(lanes == LANES - 1, 0.0, pltpu.roll(here, LANES - 1, 1))
        middle = across - 2.0 * here
        before = middle + (jnp.where(rows == 0, 0.0, pltpu.roll(here, 1, 0)) - here)
        after = middle + (jnp.where(rows == 31, 0.0, pltpu.roll(here, 31, 0)) - here)
        down = wide[coarse] - here
        up = wide[coarse + 2] - here
        for f in range(4):
            for j in range(4):
                term = (before, middle, middle, after)[j]
                if f == 0:
                    term = term + down
                if f == 3:
                    term = term + up
                at = (4 * coarse + f, pl.ds(j, 32, stride=4), slice(None))
                next_ref[at] = base_ref[at] + term


def finish(base, wide, rows, edge, guess):
    operands = [base, wide, rows] + ([] if edge is None else [edge])
    return pl.pallas_call(
        finish_kernel,
        out_shape=(
            jax.ShapeDtypeStruct(base.shape, jnp.float32),
            jax.ShapeDtypeStruct(guess.shape, jnp.float32),
        ),
        in_specs=[VMEM] * len(operands),
        out_specs=(VMEM, VMEM),
        cost_estimate=pl.CostEstimate(flops=500_000, bytes_accessed=1_100_000, transcendentals=0),
        compiler_params=PARAMS,
        name="finish",
    )(*operands)


def swaps(count, first=0):
    return [p for i in range(first, count - 1, 2) for p in ((i, i + 1), (i + 1, i))]


def per_device(comp, guess):
    slabs, groups = lax.axis_size("slab"), lax.axis_size("grp")
    group = lax.axis_index("grp")
    both = ("slab", "grp")
    devices = slabs * groups
    quads = groups // 2

    message, first, second = pack(comp, guess)

    bundle = jnp.zeros((groups,) + message.shape, jnp.float32)
    bundle = lax.dynamic_update_slice(bundle, message[None], (group, 0, 0))
    for k in range(1, groups):
        block = lax.ppermute(message, "grp", [(i, i ^ k) for i in range(groups)])
        bundle = lax.dynamic_update_slice(bundle, block[None], (group ^ k, 0, 0))

    first = lax.ppermute(first, both, swaps(devices))
    second = lax.ppermute(second, both, swaps(devices, 1))

    core = lax.ppermute(bundle, "slab", swaps(slabs))
    chip = lax.ppermute(bundle, "slab", swaps(slabs, 1))
    edge = None
    if quads < HALO:
        pairs = []
        for i in range(slabs - 2):
            pairs.append((i * groups, (i + 2) * groups))
            pairs.append(((i + 2) * groups + groups - 1, i * groups + groups - 1))
        edge = lax.ppermute(edge_of(bundle), both, pairs)

    base = base_of(comp, first, second)
    wide, rows = solve(bundle, core, chip, guess, edge is not None)
    return finish(base, wide, rows, edge, guess)


def solution(mesh):
    placed = (P(("slab", "grp"), None, None), P("slab", "grp", None))
    return jax.shard_map(per_device, mesh=mesh, in_specs=placed, out_specs=placed, check_vma=False)
```

time: 27.7 us -> 22.2 us (0.80)
  Pallas kernels: 7.91 us -> 3.67 us
  local copies, waits for them, and re-layouts: 3.24 us -> 1.83 us
  waiting for transfers between devices: 0.55 us -> 1.01 us
  starting transfers between devices: 15 us -> 14.6 us
    pallas_call x1, Pallas kernels: 2.66 us -> 0.74 us  [base_of(): pl.pallas_call(base_kernel, out_shape=jax.ShapeDtypeStruct(comp.shape, jn...]
    pallas_call x1, Pallas kernels: 1.84 us -> 0.19 us  [pack(): pl.pallas_call(pack_kernel, out_shape=(message, outer, outer), in_specs=[...]
    unnamed x14 -> x6, local copies, waits for them, and re-layouts: 3.22 us -> 1.8 us
    pallas_call x1 -> x4, Pallas kernels: 3.41 us -> 2.74 us  [the longest x1 1.36 us: solve(): pl.pallas_call(functools.partial(solve_kernel, edged), out_shape=(jax.Sha...]
    ppermute x8, waiting for transfers between devices: 0.55 us -> 1.01 us  [the longest x3 1 us: per_device(): block = lax.ppermute(message, 'grp', [(i, i ^ k) for i in range(groups)])]
    ppermute x8, starting transfers between devices: 15 us -> 14.6 us  [the longest x3 4.63 us: per_device(): block = lax.ppermute(message, 'grp', [(i, i ^ k) for i in range(groups)])]
  transfers between devices with their start and end apart: 8 -> 8, of which waited for: 1 -> 1; matrix products, arithmetic and copies ran while one was open for 0% -> 0% of each run, Pallas kernels for 10% -> 11%
where the time goes in v2:
time: 22.2 us; the launch traced here: 21.9 us
  starting transfers between devices  14.6 us (66%)
  Pallas kernels  3.67 us (17%)
  local copies, waits for them, and re-layouts  1.83 us (8%)
  waiting for transfers between devices  1.01 us (5%)
  between operations  0.79 us (4%)
    ppermute x3, starting transfers between devices, per_device(): block = lax.ppermute(message, 'grp', [(i, i ^ k) for i in range(groups)])  4.63 us
    ppermute x1, starting transfers between devices, per_device(): edge = lax.ppermute(edge_of(bundle), both, pairs)  3.48 us
    ppermute x1, starting transfers between devices, per_device(): core = lax.ppermute(bundle, 'slab', swaps(slabs))  3.29 us
    ppermute x1, starting transfers between devices, per_device(): first = lax.ppermute(first, both, swaps(devices))  1.89 us
    unnamed x6, local copies, waits for them, and re-layouts  1.8 us
    pallas_call x1, Pallas kernels, solve(): pl.pallas_call(functools.partial(solve_kernel, edged), out_shape=(jax.Sha...  1.36 us
    ppermute x3, waiting for transfers between devices, per_device(): block = lax.ppermute(message, 'grp', [(i, i ^ k) for i in range(groups)])  1 us
    pallas_call x1, Pallas kernels, finish(): pl.pallas_call(finish_kernel, out_shape=(jax.ShapeDtypeStruct(base.shape,...  0.92 us
  transfers between devices with their start and end apart: 8, of which 1 were waited for; matrix products, arithmetic and copies ran while one was open for 0% of the time, Pallas kernels for 11%

profile of v2, /device:TPU:0, one launch (start us, length us, event | category | flops | bytes accessed | tf_op | source)
XLA Modules:
  0.0 21.9 jit_solution(12525272770950898183)
XLA Ops:
  0.6 0.0 copy-start.2
  0.6 0.7 %copy-done.2 = f32[8,8,32]{2,1,0:T(8,128)S(1)} copy-done((f32[8,8,32]{2,1,0:T(8,128)S(1)}, f32[8,8,32]{2,1,0:T(8,128)}, u32[]{:S(2)}) %copy-start.2) | copy-done | bytes 8216
  1.4 0.1 pack_guess.1.guess_ref
  1.5 0.0 copy-start
  1.5 1.0 %copy-done = f32[8,128,128]{2,1,0:T(8,128)S(1)} copy-done((f32[8,128,128]{2,1,0:T(8,128)S(1)}, f32[8,128,128]{2,1,0:T(8,128)}, u32[]{:S(2)}) %copy-start) | copy-done | bytes 524312
  2.5 0.0 copy-start.1
  2.5 0.2 pack.1
  2.7 4.0 %collective-permute-start.4 = (f32[32,128]{1,0:T(8,128)S(1)}, f32[32,128]{1,0:T(8,128)S(1)}, u32[]{:S(2)}, u32[]{:S(2)}) collective-permute-start(f32[32,128]{1,0:T(8,128)S(1)} %get-tuple-element.9), channel_id=1, source_target_pairs={{0,3},{1,2},{2,1},{3,0},{4,7},{5,6},{6,5},{7,4},{8,11},{9,10},{10,... | collective-permute-start | bytes 49160 | tf_op jit(solution)/shard_map/ppermute | solution.py:433
  6.7 0.5 %collective-permute-start.3 = (f32[32,128]{1,0:T(8,128)S(1)}, f32[32,128]{1,0:T(8,128)S(1)}, u32[]{:S(2)}, u32[]{:S(2)}) collective-permute-start(f32[32,128]{1,0:T(8,128)S(1)} %get-tuple-element.9), channel_id=1, source_target_pairs={{0,2},{1,3},{2,0},{3,1},{4,6},{5,7},{6,4},{7,5},{8,10},{9,11},{10,... | collective-permute-start | bytes 49160 | tf_op jit(solution)/shard_map/ppermute | solution.py:433
  7.2 0.1 collective-permute-start.2
  7.3 1.9 %collective-permute-start = (f32[2,128,128]{2,1,0:T(8,128)S(1)}, f32[2,128,128]{2,1,0:T(8,128)S(1)}, u32[]{:S(2)}, u32[]{:S(2)}) collective-permute-start(f32[2,128,128]{2,1,0:T(8,128)S(1)} %get-tuple-element.7), channel_id=1, source_target_pairs={{0,1},{1,0},{2,3},{3,2},{4,5},{5,4},{6,7},{7,6},{8,9},{9,8},{10,11... | collective-permute-start | bytes 393224 | tf_op jit(solution)/shard_map/ppermute | solution.py:436
  9.2 0.7 %collective-permute-start.1 = (f32[2,128,128]{2,1,0:T(8,128)S(1)}, f32[2,128,128]{2,1,0:T(8,128)S(1)}, u32[]{:S(2)}, u32[]{:S(2)}) collective-permute-start(f32[2,128,128]{2,1,0:T(8,128)S(1)} %get-tuple-element.8), channel_id=1, source_target_pairs={{1,2},{2,1},{3,4},{4,3},{5,6},{6,5},{7,8},{8,7},{9,10},{10,9},{11,... | collective-permute-start | bytes 393224 | tf_op jit(solution)/shard_map/ppermute | solution.py:437
  9.9 1.0 %collective-permute-done.2 = f32[32,128]{1,0:T(8,128)S(1)} collective-permute-done((f32[32,128]{1,0:T(8,128)S(1)}, f32[32,128]{1,0:T(8,128)S(1)}, u32[]{:S(2)}, u32[]{:S(2)}) %collective-permute-start.2) | collective-permute-done | bytes 16416 | tf_op jit(solution)/shard_map/ppermute | solution.py:433
  10.9 0.0 collective-permute-done.3
  11.0 0.0 collective-permute-done.4
  11.0 0.7 %collective-permute-start.6 = (f32[4,32,128]{2,1,0:T(8,128)S(1)}, f32[4,32,128]{2,1,0:T(8,128)S(1)}, u32[]{:S(2)}, u32[]{:S(2)}) collective-permute-start(f32[4,32,128]{2,1,0:T(8,128)S(1)} %bitcast_dynamic-update-slice_fusion.own_ref), channel_id=1, source_target_pairs={{4,8},{8,4},{12,16},{16,12},{20,24},{24,20},{5,9},{9,5},{13,17},{1... | collective-permute-start | bytes 196616 | tf_op jit(solution)/shard_map/ppermute | solution.py:440
  11.7 3.3 %collective-permute-start.5 = (f32[4,32,128]{2,1,0:T(8,128)S(1)}, f32[4,32,128]{2,1,0:T(8,128)S(1)}, u32[]{:S(2)}, u32[]{:S(2)}) collective-permute-start(f32[4,32,128]{2,1,0:T(8,128)S(1)} %bitcast_dynamic-update-slice_fusion.own_ref), channel_id=1, source_target_pairs={{0,4},{4,0},{8,12},{12,8},{16,20},{20,16},{24,28},{28,24},{1,5},{5... | collective-permute-start | bytes 196616 | tf_op jit(solution)/shard_map/ppermute | solution.py:439
  14.9 0.4 %edge.1 = f32[32,128]{1,0:T(8,128)S(1)} custom-call(f32[4,32,128]{2,1,0:T(8,128)S(1)} %bitcast_dynamic-update-slice_fusion.own_ref), custom_call_target="tpu_custom_call" | custom-call | flops 500000 | bytes 80000 | tf_op jit(solution)/shard_map/edge/pallas_call | solution.py:241
  15.3 3.5 %collective-permute-start.7 = (f32[32,128]{1,0:T(8,128)S(1)}, f32[32,128]{1,0:T(8,128)S(1)}, u32[]{:S(2)}, u32[]{:S(2)}) collective-permute-start(f32[32,128]{1,0:T(8,128)S(1)} %edge.1), channel_id=1, source_target_pairs={{0,8},{11,3},{4,12},{15,7},{8,16},{19,11},{12,20},{23,15},{16,24},... | collective-permute-start | bytes 49160 | tf_op jit(solution)/shard_map/ppermute | solution.py:447
  18.8 0.0 collective-permute-done.6.chip_ref
  18.8 0.0 collective-permute-done.5.core_ref
  18.8 1.4 %solve.1 = (f32[4,32,128]{2,1,0:T(8,128)S(1)}, f32[2,8,128]{2,1,0:T(8,128)S(1)}) custom-call(f32[4,32,128]{2,1,0:T(8,128)S(1)} %bitcast_dynamic-update-slice_fusion.own_ref, f32[4,32,128]{2,1,0:T(8,128)S(1)} %collective-permute-done.5.core_ref, f32[4,32,128]{2,1,0:T(8,128)S(1)} %collective-permute-done.6.chip_ref), custom_call_target="tpu_custom_call" | custom-call | flops 6000000 | bytes 500000 | tf_op jit(solution)/shard_map/solve/pallas_call | solution.py:351
  20.2 0.0 collective-permute-done.first_ref
  20.2 0.0 collective-permute-done.1.second_ref
  20.2 0.0 copy-done.1
  20.2 0.7 %base.1.base_ref = f32[8,128,128]{2,1,0:T(8,128)S(1)} custom-call(f32[8,128,128]{2,1,0:T(8,128)S(1)} %copy-done.1, f32[2,128,128]{2,1,0:T(8,128)S(1)} %collective-permute-done.first_ref, f32[2,128,128]{2,1,0:T(8,128)S(1)} %collective-permute-done.1.second_ref), custom_call_target="tpu_custom_call" | custom-call | flops 6000000 | bytes 1500000 | tf_op jit(solution)/shard_map/base/pallas_call | solution.py:142
  21.0 0.0 collective-permute-done.7.refs_0_
  21.0 0.9 %finish.1 = (f32[8,128,128]{2,1,0:T(8,128)}, f32[8,8,32]{2,1,0:T(8,128)}) custom-call(f32[8,128,128]{2,1,0:T(8,128)S(1)} %base.1.base_ref, f32[4,32,128]{2,1,0:T(8,128)S(1)} %get-tuple-element.10.wide_ref, f32[2,8,128]{2,1,0:T(8,128)S(1)} %get-tuple-element.11.rows_ref, f32[32,128]{1,0:T(8,128)S(1)} %collective-permute-done.7.refs_0_), custom_call_target="tpu_custom_call" | custom-call | flops 500000 | bytes 1100000 | tf_op jit(solution)/shard_map/finish/pallas_call | solution.py:403
  (5 shorter events, 0.0 us)
Async XLA Ops:
  0.6 0.8 %copy-start.2 = (f32[8,8,32]{2,1,0:T(8,128)S(1)}, f32[8,8,32]{2,1,0:T(8,128)}, u32[]{:S(2)}) copy-start(f32[8,8,32]{2,1,0:T(8,128)} %guess_ref.1) | copy-start | bytes 24580
  1.5 1.0 %copy-start = (f32[8,128,128]{2,1,0:T(8,128)S(1)}, f32[8,128,128]{2,1,0:T(8,128)}, u32[]{:S(2)}) copy-start(f32[8,128,128]{2,1,0:T(8,128)} %comp_ref.3) | copy-start | bytes 1572868
  2.5 17.7 %copy-start.1 = (f32[8,128,128]{2,1,0:T(8,128)S(1)}, f32[8,128,128]{2,1,0:T(8,128)}, u32[]{:S(2)}) copy-start(f32[8,128,128]{2,1,0:T(8,128)} %comp_ref.3) | copy-start | bytes 1572868
  2.7 8.3 %collective-permute-start.4 = (f32[32,128]{1,0:T(8,128)S(1)}, f32[32,128]{1,0:T(8,128)S(1)}, u32[]{:S(2)}, u32[]{:S(2)}) collective-permute-start(f32[32,128]{1,0:T(8,128)S(1)} %get-tuple-element.9), channel_id=1, source_target_pairs={{0,3},{1,2},{2,1},{3,0},{4,7},{5,6},{6,5},{7,4},{8,11},{9,10},{10,... | collective-permute-start | bytes 49160 | tf_op jit(solution)/shard_map/ppermute | solution.py:433
  6.7 4.3 %collective-permute-start.3 = (f32[32,128]{1,0:T(8,128)S(1)}, f32[32,128]{1,0:T(8,128)S(1)}, u32[]{:S(2)}, u32[]{:S(2)}) collective-permute-start(f32[32,128]{1,0:T(8,128)S(1)} %get-tuple-element.9), channel_id=1, source_target_pairs={{0,2},{1,3},{2,0},{3,1},{4,6},{5,7},{6,4},{7,5},{8,10},{9,11},{10,... | collective-permute-start | bytes 49160 | tf_op jit(solution)/shard_map/ppermute | solution.py:433
  7.2 3.7 %collective-permute-start.2 = (f32[32,128]{1,0:T(8,128)S(1)}, f32[32,128]{1,0:T(8,128)S(1)}, u32[]{:S(2)}, u32[]{:S(2)}) collective-permute-start(f32[32,128]{1,0:T(8,128)S(1)} %get-tuple-element.9), channel_id=1, source_target_pairs={{0,1},{1,0},{2,3},{3,2},{4,5},{5,4},{6,7},{7,6},{8,9},{9,8},{10,11... | collective-permute-start | bytes 49160 | tf_op jit(solution)/shard_map/ppermute | solution.py:433
  7.3 12.9 %collective-permute-start = (f32[2,128,128]{2,1,0:T(8,128)S(1)}, f32[2,128,128]{2,1,0:T(8,128)S(1)}, u32[]{:S(2)}, u32[]{:S(2)}) collective-permute-start(f32[2,128,128]{2,1,0:T(8,128)S(1)} %get-tuple-element.7), channel_id=1, source_target_pairs={{0,1},{1,0},{2,3},{3,2},{4,5},{5,4},{6,7},{7,6},{8,9},{9,8},{10,11... | collective-permute-start | bytes 393224 | tf_op jit(solution)/shard_map/ppermute | solution.py:436
  9.2 11.0 %collective-permute-start.1 = (f32[2,128,128]{2,1,0:T(8,128)S(1)}, f32[2,128,128]{2,1,0:T(8,128)S(1)}, u32[]{:S(2)}, u32[]{:S(2)}) collective-permute-start(f32[2,128,128]{2,1,0:T(8,128)S(1)} %get-tuple-element.8), channel_id=1, source_target_pairs={{1,2},{2,1},{3,4},{4,3},{5,6},{6,5},{7,8},{8,7},{9,10},{10,9},{11,... | collective-permute-start | bytes 393224 | tf_op jit(solution)/shard_map/ppermute | solution.py:437
  11.0 7.8 %collective-permute-start.6 = (f32[4,32,128]{2,1,0:T(8,128)S(1)}, f32[4,32,128]{2,1,0:T(8,128)S(1)}, u32[]{:S(2)}, u32[]{:S(2)}) collective-permute-start(f32[4,32,128]{2,1,0:T(8,128)S(1)} %bitcast_dynamic-update-slice_fusion.own_ref), channel_id=1, source_target_pairs={{4,8},{8,4},{12,16},{16,12},{20,24},{24,20},{5,9},{9,5},{13,17},{1... | collective-permute-start | bytes 196616 | tf_op jit(solution)/shard_map/ppermute | solution.py:440
  11.7 7.2 %collective-permute-start.5 = (f32[4,32,128]{2,1,0:T(8,128)S(1)}, f32[4,32,128]{2,1,0:T(8,128)S(1)}, u32[]{:S(2)}, u32[]{:S(2)}) collective-permute-start(f32[4,32,128]{2,1,0:T(8,128)S(1)} %bitcast_dynamic-update-slice_fusion.own_ref), channel_id=1, source_target_pairs={{0,4},{4,0},{8,12},{12,8},{16,20},{20,16},{24,28},{28,24},{1,5},{5... | collective-permute-start | bytes 196616 | tf_op jit(solution)/shard_map/ppermute | solution.py:439
  15.3 5.7 %collective-permute-start.7 = (f32[32,128]{1,0:T(8,128)S(1)}, f32[32,128]{1,0:T(8,128)S(1)}, u32[]{:S(2)}, u32[]{:S(2)}) collective-permute-start(f32[32,128]{1,0:T(8,128)S(1)} %edge.1), channel_id=1, source_target_pairs={{0,8},{11,3},{4,12},{15,7},{8,16},{19,11},{12,20},{23,15},{16,24},... | collective-permute-start | bytes 49160 | tf_op jit(solution)/shard_map/ppermute | solution.py:447
